TPU v7x, 8 devices: a whole 2x2x1 slice. The times are simulated.
8 devices in a mesh: dp: 1 (over z), tp: 2 (over y), sp: 4 (over x, core).
Axes of the slice: x: 2, y: 2, z: 1, core: 2. Of those that a mesh axis runs over, the one named last changes fastest.
Arguments:
- x: bfloat16 [4096, 3584], P(('dp', 'sp'))
- pos: int32 [4096], P(('dp', 'sp'))
- k_hist: bfloat16 [3, 8192, 4, 128], P(None, ('dp', 'sp'), 'tp')
- v_hist: bfloat16 [3, 8192, 4, 128], P(None, ('dp', 'sp'), 'tp')
- wq: bfloat16 [3, 3584, 3584], P(None, None, 'tp')
- wk: bfloat16 [3, 3584, 512], P(None, None, 'tp')
- wv: bfloat16 [3, 3584, 512], P(None, None, 'tp')
- wo: bfloat16 [3, 3584, 3584], P(None, 'tp')
- wg: bfloat16 [3, 3584, 18944], P(None, None, 'tp')
- wu: bfloat16 [3, 3584, 18944], P(None, None, 'tp')
- wd: bfloat16 [3, 18944, 3584], P(None, 'tp')
- g1: bfloat16 [3, 3584], replicated
- g2: bfloat16 [3, 3584], replicated
Outputs:
- output 1: bfloat16 [4096, 3584], P(('dp', 'sp'))
- output 2: bfloat16 [3, 4096, 4, 128], P(None, ('dp', 'sp'), 'tp')
- output 3: bfloat16 [3, 4096, 4, 128], P(None, ('dp', 'sp'), 'tp')
All inputs are finite; a program needn't handle non-finite values.
Results may differ from a plain program's by a relative error of at most 0.02.
Values are sent between devices in bfloat16 or wider.
A program may use at most 2.75 GiB of HBM per device.

v0:
```python
import jax
import jax.numpy as jnp
from jax import lax
from jax.sharding import PartitionSpec as P

EPS = 1e-5
ROPE_THETA = 500000.0
QB = 64


def rmsnorm(x, g):
    xf = x.astype(jnp.float32)
    r = lax.rsqrt(jnp.mean(xf * xf, axis=-1, keepdims=True) + EPS)
    return (xf * r * g.astype(jnp.float32)).astype(jnp.bfloat16)


def rope(t, pos):
    half = t.shape[-1] // 2
    inv = ROPE_THETA ** (-(jnp.arange(half, dtype=jnp.float32) * (2.0 / t.shape[-1])))
    ang = pos.astype(jnp.float32)[..., None] * inv
    c = jnp.cos(ang)[..., None, :]
    s = jnp.sin(ang)[..., None, :]
    tf = t.astype(jnp.float32)
    t1 = tf[..., :half]
    t2 = tf[..., half:]
    return jnp.concatenate([t1 * c - t2 * s, t2 * c + t1 * s], axis=-1).astype(jnp.bfloat16)


def mm(a, b):
    return jnp.dot(a, b, preferred_element_type=jnp.float32)


def partial_attn(qq, k, v, mask=None):
    s = jnp.einsum('qkgd,tkd->qkgt', qq, k, preferred_element_type=jnp.float32) * (k.shape[-1] ** -0.5)
    if mask is not None:
        s = jnp.where(mask, s, -jnp.inf)
    m = jnp.max(s, axis=-1)
    p = jnp.exp(s - m[..., None])
    o = jnp.einsum('qkgt,tkd->qkgd', p.astype(jnp.bfloat16), v, preferred_element_type=jnp.float32)
    return m, jnp.sum(p, axis=-1), o


def solution(mesh):
    sp = mesh.shape['sp']
    row = ('dp', 'sp')
    kv_spec = P(None, row, 'tp', None)
    col = P(None, None, 'tp')
    rowsplit = P(None, 'tp', None)

    def body(x, pos, k_hist, v_hist, wq, wk, wv, wo, wg, wu, wd, g1, g2):
        n, d = x.shape
        layers, _, kvl, dh = k_hist.shape
        hql = wq.shape[-1] // dh
        g = hql // kvl
        s_tot = n * sp
        idx = lax.axis_index('sp')
        kpos = jnp.arange(s_tot)
        starts = idx * n + jnp.arange(n // QB) * QB
        ks, vs = [], []
        for l in range(layers):
            h = rmsnorm(x, g1[l])
            q = rope(mm(h, wq[l]).astype(jnp.bfloat16).reshape(n, hql, dh), pos)
            k = rope(mm(h, wk[l]).astype(jnp.bfloat16).reshape(n, kvl, dh), pos)
            v = mm(h, wv[l]).astype(jnp.bfloat16).reshape(n, kvl, dh)
            ks.append(k)
            vs.append(v)

            q_all = lax.all_gather(q, 'sp', axis=0, tiled=True).reshape(s_tot // QB, QB, kvl, g, dh)
            kh = k_hist[l]
            vh = v_hist[l]
            m_h, l_h, o_h = lax.map(lambda qq: partial_attn(qq, kh, vh), q_all)
            m_h = m_h.reshape(s_tot, kvl, g)
            m_g = lax.pmax(m_h, 'sp')
            sc = jnp.exp(m_h - m_g)
            o_h = lax.psum_scatter(o_h.reshape(s_tot, kvl, g, dh) * sc[..., None], 'sp', scatter_dimension=0, tiled=True)
            l_h = lax.psum_scatter(l_h.reshape(s_tot, kvl, g) * sc, 'sp', scatter_dimension=0, tiled=True)
            m_h = lax.dynamic_slice_in_dim(m_g, idx * n, n, axis=0)

            k_all = lax.all_gather(k, 'sp', axis=0, tiled=True)
            v_all = lax.all_gather(v, 'sp', axis=0, tiled=True)

            def new_blk(args, k_all=k_all, v_all=v_all):
                st, qq = args
                mask = (kpos[None, :] <= (st + jnp.arange(QB))[:, None])[:, None, None, :]
                return partial_attn(qq, k_all, v_all, mask)

            m_n, l_n, o_n = lax.map(new_blk, (starts, q.reshape(n // QB, QB, kvl, g, dh)))
            m_n = m_n.reshape(n, kvl, g)
            l_n = l_n.reshape(n, kvl, g)
            o_n = o_n.reshape(n, kvl, g, dh)
            mt = jnp.maximum(m_h, m_n)
            a_h = jnp.exp(m_h - mt)
            a_n = jnp.exp(m_n - mt)
            den = l_h * a_h + l_n * a_n
            o = (o_h * a_h[..., None] + o_n * a_n[..., None]) / den[..., None]
            attn = o.astype(jnp.bfloat16).reshape(n, hql * dh)
            x = x + lax.psum(mm(attn, wo[l]), 'tp').astype(jnp.bfloat16)

            h2 = rmsnorm(x, g2[l])
            a = mm(h2, wg[l]).astype(jnp.bfloat16)
            b = mm(h2, wu[l]).astype(jnp.bfloat16)
            u = (jax.nn.silu(a.astype(jnp.float32)) * b.astype(jnp.float32)).astype(jnp.bfloat16)
            x = x + lax.psum(mm(u, wd[l]), 'tp').astype(jnp.bfloat16)
        return x, jnp.stack(ks), jnp.stack(vs)

    in_specs = (P(row, None), P(row), kv_spec, kv_spec, col, col, col, rowsplit, col, col, rowsplit, P(), P())
    out_specs = (P(row, None), kv_spec, kv_spec)
    return jax.shard_map(body, mesh=mesh, in_specs=in_specs, out_specs=out_specs, check_vma=False)
```

profile of v0, /device:TPU:0, one launch (start us, length us, event | category | flops | bytes accessed | tf_op | source)
XLA Modules:
  0.0 6221.6 jit_solution(290239571495353411)
XLA Ops:
  14.0 20.4 fusion.240
  52.4 12.0 all-gather.12.cloned.1.call-start
  87.7 59.7 all-gather.10.cloned.1.call-done
  147.5 20.1 copy.118
  167.6 13.4 broadcast.248.clone2
  181.1 370.3 %while.87 = (s32[]{:T(128)}, f32[64,64,2,7]{1,0,2,3:T(8,128)S(1)}, f32[64,64,2,7]{1,0,2,3:T(8,128)S(1)}, f32[64,64,2,7,128]{4,1,0,3,2:T(8,128)}, bf16[64,64,2,7,...) while((s32[]{:T(128)}, f32[64,64,2,7]{1,0,2,3:T(8,128)S(1)}, ...), condition=%wide.region_4.5_spmd, body=%wide.region_1.4_spmd.sunk | while | flops 954202368 | bytes 24849508 | solution.py:71
  599.5 11.2 reshape.462
  610.9 20.1 bitcast_multiply_fusion.2
  635.1 451.5 %while.90 = (s32[]{:T(128)}, f32[16,64,2,7]{1,0,2,3:T(8,128)S(1)}, f32[16,64,2,7]{1,0,2,3:T(8,128)S(1)}, f32[16,64,2,7,128]{4,1,0,3,2:T(8,128)}, s32[16]{0:T(128...) while((s32[]{:T(128)}, f32[16,64,2,7]{1,0,2,3:T(8,128)S(1)}, ...), condition=%wide.region_10.11_spmd.clone, body=%wide.region_7.10_spmd.clone.sunk | while | flops 1919678720 | bytes 58404504 | solution.py:87
  1109.3 21.0 fusion.218
  1130.3 337.2 %all-reduce.15 = bf16[1024,3584]{1,0:T(8,128)(2,1)} all-reduce(f32[1024,3584]{1,0:T(8,128)} %fusion.218), channel_id=1, replica_groups=mesh['dp'=1,'tp'=2,'sp'=4] {'tp'}, use_global_device_ids=true, to_apply=%region_12.13 | all-reduce | flops 3670016 | bytes 22020096 | tf_op jit(solution)/shard_map/psum | solution.py:97
  1467.5 11.5 fusion.195
  1479.0 84.6 %fusion.154 = bf16[1024,9472]{1,0:T(8,128)(2,1)} fusion(bf16[3,3584,9472]{2,1,0:T(8,128)(2,1)} %param.33, bf16[1024,3584]{1,0:T(8,128)(2,1)} %get-tuple-element.589, f32[3584]{0:T(1024)S(1)} %copy-done.53, f32[1024]{0:T(1024)S(1)} %add_rsqrt_fusion.4), kind=kOutput, calls=%fused_computation.130 | convolution fusion | flops 69539463168 | bytes 94652416 | tf_op jit(solution)/shard_map/dot_general | solution.py:30
  1563.6 81.1 %fusion.152 = bf16[1024,9472]{1,0:T(8,128)(2,1)} fusion(bf16[3,3584,9472]{2,1,0:T(8,128)(2,1)} %param.34, bf16[1024,3584]{1,0:T(8,128)(2,1)S(1)} %copy-done.2, f32[3584]{0:T(1024)S(1)} %copy-done.53, f32[1024]{0:T(1024)S(1)} %add_rsqrt_fusion.4), kind=kOutput, calls=%fused_computation.128 | convolution fusion | flops 69539463168 | bytes 94652416 | tf_op jit(solution)/shard_map/dot_general | solution.py:30
  1644.7 87.5 %fusion.150 = f32[1024,3584]{1,0:T(8,128)} fusion(bf16[3,9472,3584]{2,1,0:T(8,128)(2,1)} %param.35, bf16[1024,9472]{1,0:T(8,128)(2,1)} %fusion.152, bf16[1024,9472]{1,0:T(8,128)(2,1)} %fusion.154), kind=kOutput, calls=%fused_computation.126 | convolution fusion | flops 69602377728 | bytes 121372672 | tf_op jit(solution)/shard_map/dot_general | solution.py:30
  1732.3 333.7 %all-reduce.16 = bf16[1024,3584]{1,0:T(8,128)(2,1)} all-reduce(f32[1024,3584]{1,0:T(8,128)} %fusion.150), channel_id=1, replica_groups=mesh['dp'=1,'tp'=2,'sp'=4] {'tp'}, use_global_device_ids=true, to_apply=%region_14.15 | all-reduce | flops 3670016 | bytes 22020096 | tf_op jit(solution)/shard_map/psum | solution.py:103
  2066.0 11.3 fusion.198
  2077.4 21.1 fusion.246
  2134.1 73.0 %all-gather.16.cloned.1.call-done = bf16[4096,14,128]{0,2,1:T(8,128)(2,1)} async-done(((bf16[1024,14,128]{0,2,1:T(8,128)(2,1)}), bf16[4096,14,128]{0,2,1:T(8,128)(2,1)}) %all-gather.16.cloned.1.call-update) | async-done | bytes 14680080 | tf_op jit(solution)/shard_map/all_gather | solution.py:68
  2207.2 20.1 copy.141
  2227.3 13.4 broadcast.248.clone2.1
  2240.8 370.3 %while.88 = (s32[]{:T(128)}, f32[64,64,2,7]{1,0,2,3:T(8,128)S(1)}, f32[64,64,2,7]{1,0,2,3:T(8,128)S(1)}, f32[64,64,2,7,128]{4,1,0,3,2:T(8,128)}, bf16[64,64,2,7,...) while((s32[]{:T(128)}, f32[64,64,2,7]{1,0,2,3:T(8,128)S(1)}, ...), condition=%wide.region_19.20_spmd, body=%wide.region_16.19_spmd.sunk | while | flops 954202368 | bytes 24849508 | solution.py:71
  2658.4 11.2 reshape.464
  2669.8 20.1 bitcast_multiply_fusion.1
  2694.0 453.2 %while.91 = (s32[]{:T(128)}, f32[16,64,2,7]{1,0,2,3:T(8,128)S(1)}, f32[16,64,2,7]{1,0,2,3:T(8,128)S(1)}, f32[16,64,2,7,128]{4,1,0,3,2:T(8,128)}, s32[16]{0:T(128...) while((s32[]{:T(128)}, f32[16,64,2,7]{1,0,2,3:T(8,128)S(1)}, ...), condition=%wide.region_25.26_spmd.clone, body=%wide.region_22.25_spmd.clone.sunk | while | flops 1919678720 | bytes 58404504 | solution.py:87
  3169.8 21.0 fusion.214
  3190.8 337.2 %all-reduce.17 = bf16[1024,3584]{1,0:T(8,128)(2,1)} all-reduce(f32[1024,3584]{1,0:T(8,128)} %fusion.214), channel_id=1, replica_groups=mesh['dp'=1,'tp'=2,'sp'=4] {'tp'}, use_global_device_ids=true, to_apply=%region_27.28 | all-reduce | flops 3670016 | bytes 22020096 | tf_op jit(solution)/shard_map/psum | solution.py:97
  3528.0 11.4 fusion.201
  3539.4 84.6 %fusion.148 = bf16[1024,9472]{1,0:T(8,128)(2,1)} fusion(bf16[3,3584,9472]{2,1,0:T(8,128)(2,1)} %param.33, bf16[1024,3584]{1,0:T(8,128)(2,1)} %get-tuple-element.580, f32[3584]{0:T(1024)S(1)} %copy-done.52, f32[1024]{0:T(1024)S(1)} %add_rsqrt_fusion.2), kind=kOutput, calls=%fused_computation.124 | convolution fusion | flops 69539463168 | bytes 94652416 | tf_op jit(solution)/shard_map/dot_general | solution.py:30
  3624.0 81.1 %fusion.146 = bf16[1024,9472]{1,0:T(8,128)(2,1)} fusion(bf16[3,3584,9472]{2,1,0:T(8,128)(2,1)} %param.34, bf16[1024,3584]{1,0:T(8,128)(2,1)S(1)} %copy-done.1, f32[3584]{0:T(1024)S(1)} %copy-done.52, f32[1024]{0:T(1024)S(1)} %add_rsqrt_fusion.2), kind=kOutput, calls=%fused_computation.122 | convolution fusion | flops 69539463168 | bytes 94652416 | tf_op jit(solution)/shard_map/dot_general | solution.py:30
  3705.2 87.5 %fusion.144 = f32[1024,3584]{1,0:T(8,128)} fusion(bf16[3,9472,3584]{2,1,0:T(8,128)(2,1)} %param.35, bf16[1024,9472]{1,0:T(8,128)(2,1)} %fusion.146, bf16[1024,9472]{1,0:T(8,128)(2,1)} %fusion.148), kind=kOutput, calls=%fused_computation.120 | convolution fusion | flops 69602377728 | bytes 121372672 | tf_op jit(solution)/shard_map/dot_general | solution.py:30
  3792.7 333.8 %all-reduce.18 = bf16[1024,3584]{1,0:T(8,128)(2,1)} all-reduce(f32[1024,3584]{1,0:T(8,128)} %fusion.144), channel_id=1, replica_groups=mesh['dp'=1,'tp'=2,'sp'=4] {'tp'}, use_global_device_ids=true, to_apply=%region_29.30 | all-reduce | flops 3670016 | bytes 22020096 | tf_op jit(solution)/shard_map/psum | solution.py:103
  4126.4 11.3 fusion.204
  4137.8 21.1 fusion.252
  4194.5 73.1 %all-gather.22.cloned.1.call-done = bf16[4096,14,128]{0,2,1:T(8,128)(2,1)} async-done(((bf16[1024,14,128]{0,2,1:T(8,128)(2,1)}), bf16[4096,14,128]{0,2,1:T(8,128)(2,1)}) %all-gather.22.cloned.1.call-update) | async-done | bytes 14680080 | tf_op jit(solution)/shard_map/all_gather | solution.py:68
  4267.6 20.1 copy.162
  4287.7 13.4 broadcast.248.clone
  4301.3 370.3 %while.89 = (s32[]{:T(128)}, f32[64,64,2,7]{1,0,2,3:T(8,128)S(1)}, f32[64,64,2,7]{1,0,2,3:T(8,128)S(1)}, f32[64,64,2,7,128]{4,1,0,3,2:T(8,128)}, bf16[64,64,2,7,...) while((s32[]{:T(128)}, f32[64,64,2,7]{1,0,2,3:T(8,128)S(1)}, ...), condition=%wide.region_34.35_spmd, body=%wide.region_31.34_spmd.sunk | while | flops 954202368 | bytes 24849508 | solution.py:71
  4734.8 11.2 reshape.466
  4746.3 20.1 bitcast_multiply_fusion
  4770.4 454.5 %while.92 = (s32[]{:T(128)}, f32[16,64,2,7]{1,0,2,3:T(8,128)S(1)}, f32[16,64,2,7]{1,0,2,3:T(8,128)S(1)}, f32[16,64,2,7,128]{4,1,0,3,2:T(8,128)}, s32[16]{0:T(128...) while((s32[]{:T(128)}, f32[16,64,2,7]{1,0,2,3:T(8,128)S(1)}, ...), condition=%wide.region_40.41_spmd.clone, body=%wide.region_37.40_spmd.clone.sunk | while | flops 1919678720 | bytes 58404504 | solution.py:87
  5248.0 20.8 fusion.210
  5268.9 337.2 %all-reduce.19 = bf16[1024,3584]{1,0:T(8,128)(2,1)} all-reduce(f32[1024,3584]{1,0:T(8,128)} %fusion.210), channel_id=1, replica_groups=mesh['dp'=1,'tp'=2,'sp'=4] {'tp'}, use_global_device_ids=true, to_apply=%region_42.43 | all-reduce | flops 3670016 | bytes 22020096 | tf_op jit(solution)/shard_map/psum | solution.py:97
  5606.0 11.4 fusion.207
  5617.5 84.5 %fusion.142 = bf16[1024,9472]{1,0:T(8,128)(2,1)} fusion(bf16[3,3584,9472]{2,1,0:T(8,128)(2,1)} %param.33, bf16[1024,3584]{1,0:T(8,128)(2,1)} %get-tuple-element.571, f32[3584]{0:T(1024)S(1)} %copy-done.49, f32[1024]{0:T(1024)S(1)} %add_rsqrt_fusion), kind=kOutput, calls=%fused_computation.118 | convolution fusion | flops 69539463168 | bytes 94652416 | tf_op jit(solution)/shard_map/dot_general | solution.py:30
  5702.0 81.1 %fusion.140 = bf16[1024,9472]{1,0:T(8,128)(2,1)} fusion(bf16[3,3584,9472]{2,1,0:T(8,128)(2,1)} %param.34, bf16[1024,3584]{1,0:T(8,128)(2,1)S(1)} %copy-done.3, f32[3584]{0:T(1024)S(1)} %copy-done.49, f32[1024]{0:T(1024)S(1)} %add_rsqrt_fusion), kind=kOutput, calls=%fused_computation.116 | convolution fusion | flops 69539463168 | bytes 94652416 | tf_op jit(solution)/shard_map/dot_general | solution.py:30
  5783.1 87.5 %fusion.138 = f32[1024,3584]{1,0:T(8,128)} fusion(bf16[3,9472,3584]{2,1,0:T(8,128)(2,1)} %param.35, bf16[1024,9472]{1,0:T(8,128)(2,1)} %fusion.140, bf16[1024,9472]{1,0:T(8,128)(2,1)} %fusion.142), kind=kOutput, calls=%fused_computation.114 | convolution fusion | flops 69602377728 | bytes 121372672 | tf_op jit(solution)/shard_map/dot_general | solution.py:30
  5870.6 333.8 %all-reduce.20 = bf16[1024,3584]{1,0:T(8,128)(2,1)} all-reduce(f32[1024,3584]{1,0:T(8,128)} %fusion.138), channel_id=1, replica_groups=mesh['dp'=1,'tp'=2,'sp'=4] {'tp'}, use_global_device_ids=true, to_apply=%region_44.45 | all-reduce | flops 3670016 | bytes 22020096 | tf_op jit(solution)/shard_map/psum | solution.py:103
  (2220 shorter events, 2825.5 us)
Async XLA Ops:
  7.2 140.3 %all-gather.10.cloned.1.call-start = ((), (), s32[]{:S(2)}) async-start(), calls=%async_computation.6 | async-start | bytes 18350080 | tf_op jit(solution)/shard_map/all_gather | solution.py:68
  43.8 20.6 copy-start.19
  43.8 20.8 copy-start.22
  52.4 535.0 %all-gather.12.cloned.1.call-start = ((), (), s32[]{:S(2)}) async-start(), calls=%async_computation.9 | async-start | bytes 2621440 | tf_op jit(solution)/shard_map/all_gather | solution.py:79
  64.6 9.3 copy-start.13
  64.8 9.1 copy-start.16
  78.3 511.2 %all-reduce.10.cloned.1.call-start = ((), (), s32[]{:S(2)}) async-start(), calls=%async_computation.7 | async-start | bytes 458752 | tf_op jit(solution)/shard_map/pmax | solution.py:73
  552.4 78.8 %all-gather.14.cloned.1.call-start = ((), (), s32[]{:S(2)}) async-start(), calls=%async_computation.10 | async-start | bytes 2621440 | tf_op jit(solution)/shard_map/all_gather | solution.py:80
  558.4 18.7 copy-start.40
  559.4 527.5 %reduce-scatter.19.cloned.1.call-start = ((), (), s32[]{:S(2)}) async-start(), calls=%async_computation.21 | async-start | bytes 2621440
  577.1 9.6 copy-start.48
  577.1 12.4 copy-start.44
  610.9 483.5 %reduce-scatter.13.cloned.1.call-start = ((), (), s32[]{:S(2)}) async-start(), calls=%async_computation.8 | async-start | bytes 36700160 | tf_op jit(solution)/shard_map/reduce_scatter | solution.py:75
  631.1 1576.1 %all-gather.16.cloned.1.call-start = ((), (), s32[]{:S(2)}) async-start(), calls=%async_computation.11 | async-start | bytes 18350080 | tf_op jit(solution)/shard_map/all_gather | solution.py:68
  1086.7 16.6 copy-start.58
  1467.5 11.5 copy-start.53
  1479.0 84.6 %copy-start.2 = (bf16[1024,3584]{1,0:T(8,128)(2,1)S(1)}, bf16[1024,3584]{1,0:T(8,128)(2,1)}, u32[]{:S(2)}) copy-start(bf16[1024,3584]{1,0:T(8,128)(2,1)} %get-tuple-element.589) | copy-start | bytes 22020100
  2066.0 11.4 copy-start.51
  2115.3 531.0 %all-gather.18.cloned.1.call-start = ((), (), s32[]{:S(2)}) async-start(), calls=%async_computation.14 | async-start | bytes 2621440 | tf_op jit(solution)/shard_map/all_gather | solution.py:79
  2117.0 11.5 copy-start.14
  2117.1 11.5 copy-start.17
  2134.1 514.3 %all-reduce.12.cloned.1.call-start = ((), (), s32[]{:S(2)}) async-start(), calls=%async_computation.12 | async-start | bytes 458752 | tf_op jit(solution)/shard_map/pmax | solution.py:73
  2612.1 78.0 %all-gather.20.cloned.1.call-start = ((), (), s32[]{:S(2)}) async-start(), calls=%async_computation.15 | async-start | bytes 2621440 | tf_op jit(solution)/shard_map/all_gather | solution.py:80
  2618.5 18.2 copy-start.42
  2619.5 527.8 %reduce-scatter.21.cloned.1.call-start = ((), (), s32[]{:S(2)}) async-start(), calls=%async_computation.22 | async-start | bytes 2621440
  2636.7 11.7 copy-start.46
  2669.8 485.0 %reduce-scatter.15.cloned.1.call-start = ((), (), s32[]{:S(2)}) async-start(), calls=%async_computation.13 | async-start | bytes 36700160 | tf_op jit(solution)/shard_map/reduce_scatter | solution.py:75
  2690.0 1577.6 %all-gather.22.cloned.1.call-start = ((), (), s32[]{:S(2)}) async-start(), calls=%async_computation.16 | async-start | bytes 18350080 | tf_op jit(solution)/shard_map/all_gather | solution.py:68
  3528.0 11.4 copy-start.52
  3539.4 84.6 %copy-start.1 = (bf16[1024,3584]{1,0:T(8,128)(2,1)S(1)}, bf16[1024,3584]{1,0:T(8,128)(2,1)}, u32[]{:S(2)}) copy-start(bf16[1024,3584]{1,0:T(8,128)(2,1)} %get-tuple-element.580) | copy-start | bytes 22020100
  4126.4 11.4 copy-start.50
  4175.7 545.9 %all-gather.24.cloned.1.call-start = ((), (), s32[]{:S(2)}) async-start(), calls=%async_computation.19 | async-start | bytes 2621440 | tf_op jit(solution)/shard_map/all_gather | solution.py:79
  4177.5 11.5 copy-start.15
  4177.5 11.5 copy-start.18
  4194.5 530.2 %all-reduce.14.cloned.1.call-start = ((), (), s32[]{:S(2)}) async-start(), calls=%async_computation.17 | async-start | bytes 458752 | tf_op jit(solution)/shard_map/pmax | solution.py:73
  4672.5 94.0 %all-gather.26.cloned.1.call-start = ((), (), s32[]{:S(2)}) async-start(), calls=%async_computation.20 | async-start | bytes 2621440 | tf_op jit(solution)/shard_map/all_gather | solution.py:80
  4679.0 9.3 copy-start.5
  4680.1 545.1 %reduce-scatter.23.cloned.1.call-start = ((), (), s32[]{:S(2)}) async-start(), calls=%async_computation.23 | async-start | bytes 2621440
  4700.5 14.7 copy-start.26
  4700.5 14.7 copy-start.28
  4700.5 14.7 copy-start.30
  4700.5 14.7 copy-start.32
  4700.5 14.7 copy-start.34
  4700.5 14.7 copy-start.36
  4710.2 14.5 copy-start.45
  4746.1 486.9 %reduce-scatter.17.cloned.1.call-start = ((), (), s32[]{:S(2)}) async-start(), calls=%async_computation.18 | async-start | bytes 36700160 | tf_op jit(solution)/shard_map/reduce_scatter | solution.py:75
  5606.0 11.4 copy-start.49
  5617.5 84.5 %copy-start.3 = (bf16[1024,3584]{1,0:T(8,128)(2,1)S(1)}, bf16[1024,3584]{1,0:T(8,128)(2,1)}, u32[]{:S(2)}) copy-start(bf16[1024,3584]{1,0:T(8,128)(2,1)} %get-tuple-element.571) | copy-start | bytes 22020100
  (76 other events, 539.9 us)
Sparse Core Ops, SparseCore 0:
  52.5 94.9 all-gather.9
  149.0 19.5 all-gather.11
  552.5 26.5 all-reduce.9
  580.5 19.5 all-gather.13
  611.0 25.5 reduce-scatter.18
  639.0 194.1 reduce-scatter.12
  2115.4 91.7 all-gather.15
  2209.3 19.5 all-gather.17
  2612.2 26.5 all-reduce.11
  2640.2 19.5 all-gather.19
  2669.9 25.4 reduce-scatter.20
  2697.8 194.1 reduce-scatter.14
  4175.8 91.7 all-gather.21
  4269.0 19.5 all-gather.23
  4672.6 26.5 all-reduce.13
  4700.6 19.5 all-gather.25
  4746.2 25.4 reduce-scatter.22
  4774.2 194.1 reduce-scatter.16
where the time goes:
time: 6240 us; the launch traced here: 6220 us
  matrix products  2590 us (42%)
  blocking collectives  2010 us (32%)
  other arithmetic  965 us (15%)
  local copies, waits for them, and re-layouts  405 us (6%)
  waiting for transfers between devices  206 us (3%)
    psum x3, blocking collectives, body(): x = x + lax.psum(mm(attn, wo[l]), 'tp').astype(jnp.bfloat16)  1010 us
    psum x3, blocking collectives, body(): x = x + lax.psum(mm(u, wd[l]), 'tp').astype(jnp.bfloat16)  1000 us
    dot_general x21, matrix products, mm(): return jnp.dot(a, b, preferred_element_type=jnp.float32)  921 us
    dot_general x240, matrix products, partial_attn(): jnp.einsum('qkgt,tkd->qkgd', p.astype(jnp.bfloat16), v, preferred_element...  835 us
    dot_general x240, matrix products, partial_attn(): jnp.einsum('qkgd,tkd->qkgt', qq, k, preferred_element_type=jnp.float32)  833 us
    reduce_sum x240, other arithmetic, partial_attn(): return (m, jnp.sum(p, axis=-1), o)  689 us
    all_gather x3, waiting for transfers between devices, body(): lax.all_gather(q, 'sp', axis=0, tiled=True)  206 us
    unnamed x140, local copies, waits for them, and re-layouts  133 us
  transfers between devices with their start and end apart: 18, of which 3 were waited for; matrix products, arithmetic and copies ran while one was open for 47% of the time, Pallas kernels for 0%

commit v1 on v0

v1 whole, which is shorter than its diff:
```python
import functools

import jax
import jax.numpy as jnp
from jax import lax
from jax.experimental import pallas as pl
from jax.experimental.pallas import tpu as pltpu
from jax.sharding import PartitionSpec as P

EPS = 1e-5
ROPE_THETA = 500000.0
LOG2E = 1.4426950408889634
NT = (((1,), (1,)), ((), ()))
F32 = jnp.float32
BF16 = jnp.bfloat16
VMEM_LIMIT = 60 * 2**20
TB = 256
CB = 256
OB = 512
DB = 512
HCHUNK = 2048
UNROLL = 3


def params(n=1):
    return pltpu.CompilerParams(vmem_limit_bytes=VMEM_LIMIT, dimension_semantics=("arbitrary",) * n)


def cost(flops, nbytes):
    return pl.CostEstimate(flops=int(flops), bytes_accessed=int(nbytes), transcendentals=0)


def norm_into(h_ref, x_ref, g_ref):
    xf = x_ref[...].astype(F32)
    r = lax.rsqrt(jnp.mean(xf * xf, axis=-1, keepdims=True) + EPS)
    h_ref[...] = (xf * r * g_ref[0].astype(F32)).astype(BF16)


def qkv_kernel(x_ref, g_ref, cos_ref, sin_ref, wq_ref, wk_ref, wv_ref, q_ref, kv_ref, h_ref, *, dh, nk):
    i = pl.program_id(0)

    def rope(t):
        t = t.astype(BF16).astype(F32)
        return (t * cos_ref[...] + pltpu.roll(t, dh // 2, 1) * sin_ref[...]).astype(BF16)

    @pl.when(i == 0)
    def _():
        norm_into(h_ref, x_ref, g_ref)
        y = jnp.dot(h_ref[...], wk_ref[0], preferred_element_type=F32)
        z = jnp.dot(h_ref[...], wv_ref[0], preferred_element_type=F32)
        for j in range(nk):
            kv_ref[0, j] = rope(y[:, j * dh:(j + 1) * dh])
            kv_ref[1, j] = z[:, j * dh:(j + 1) * dh].astype(BF16)

    @pl.when(i > 0)
    def _():
        y = jnp.dot(h_ref[...], wq_ref[0], preferred_element_type=F32)
        for j in range(CB // dh):
            q_ref[j] = rope(y[:, j * dh:(j + 1) * dh])


def qkv(l, x, g, cos, sin, wq, wk, wv, dh):
    n, d = x.shape
    cq, ck = wq.shape[-1], wk.shape[-1]
    nk = ck // dh
    nb = cq // CB
    qi = lambda i: jnp.maximum(i - 1, 0)
    return pl.pallas_call(
        functools.partial(qkv_kernel, dh=dh, nk=nk),
        grid=(nb + 1,),
        in_specs=[
            pl.BlockSpec((n, d), lambda i: (0, 0)),
            pl.BlockSpec((1, 1, d), lambda i: (l, 0, 0)),
            pl.BlockSpec((n, dh), lambda i: (0, 0)),
            pl.BlockSpec((n, dh), lambda i: (0, 0)),
            pl.BlockSpec((1, d, CB), lambda i: (l, 0, qi(i))),
            pl.BlockSpec((1, d, ck), lambda i: (l, 0, 0)),
            pl.BlockSpec((1, d, ck), lambda i: (l, 0, 0)),
        ],
        out_specs=[
            pl.BlockSpec((CB // dh, n, dh), lambda i: (qi(i), 0, 0)),
            pl.BlockSpec((2, nk, n, dh), lambda i: (0, 0, 0, 0)),
        ],
        out_shape=[
            jax.ShapeDtypeStruct((cq // dh, n, dh), BF16),
            jax.ShapeDtypeStruct((2, nk, n, dh), BF16),
        ],
        scratch_shapes=[pltpu.VMEM((n, d), BF16)],
        compiler_params=params(),
        cost_estimate=cost(2 * n * d * (cq + 2 * ck), 2 * d * (cq + 2 * ck)),
        name='qkv',
    )(x, g, cos, sin, wq, wk, wv)


def softmax_step(q, k, v, m_ref, l_ref, acc_ref, c, first=False, mask=None):
    s = lax.dot_general(q, k, NT, preferred_element_type=F32)
    if mask is not None:
        s = jnp.where(mask, s, -jnp.inf)
    dh = acc_ref.shape[-1]
    shape = acc_ref.shape
    rows = s.shape[0]
    mx = jnp.max(s, axis=1, keepdims=True)
    if first:
        mn = jnp.broadcast_to(mx, (rows, dh))
    else:
        mp = m_ref[...].reshape(rows, dh)
        mn = jnp.maximum(mp, mx)
        a = jnp.exp2((mp - mn) * c)
    m_ref[...] = mn.reshape(shape)
    nb = s.shape[1] // dh
    p = jnp.exp2((s - jnp.concatenate([mn] * nb, axis=1)) * c)
    ls = p[:, :dh]
    for b in range(1, nb):
        ls = ls + p[:, b * dh:(b + 1) * dh]
    o = jnp.dot(p.astype(BF16), v, preferred_element_type=F32)
    if not first:
        ls = l_ref[...].reshape(rows, dh) * a + ls
        o = acc_ref[...].reshape(rows, dh) * a + o
    l_ref[...] = ls.reshape(shape)
    acc_ref[...] = o.reshape(shape)


def hist_kernel(q_ref, k_ref, v_ref, m_ref, l_ref, acc_ref, *, c, chunk):
    g, tb, dh = q_ref.shape
    q = q_ref[...].reshape(g * tb, dh)
    for_sp, per = k_ref.shape[0], k_ref.shape[3] // chunk
    softmax_step(q, k_ref[0, 0, 0, :chunk], v_ref[0, 0, 0, :chunk], m_ref, l_ref, acc_ref, c, first=True)

    def body(j, _):
        a = j // per
        rows = pl.ds(pl.multiple_of((j - a * per) * chunk, chunk), chunk)
        softmax_step(q, k_ref[a, 0, 0, rows], v_ref[a, 0, 0, rows], m_ref, l_ref, acc_ref, c)
        return 0

    lax.fori_loop(1, for_sp * per, body, 0, unroll=UNROLL)


def hist_attn(q, kv, c):
    hq, n, dh = q.shape
    sp, _, nk, t, _ = kv.shape
    g = hq // nk
    st = pl.BlockSpec((g, TB, dh), lambda h, i: (h, i, 0))
    sd = jax.ShapeDtypeStruct((hq, n, dh), F32)
    return pl.pallas_call(
        functools.partial(hist_kernel, c=c, chunk=min(HCHUNK, t)),
        grid=(nk, n // TB),
        in_specs=[
            st,
            pl.BlockSpec((sp, 1, 1, t, dh), lambda h, i: (0, 0, h, 0, 0)),
            pl.BlockSpec((sp, 1, 1, t, dh), lambda h, i: (0, 1, h, 0, 0)),
        ],
        out_specs=[st, st, st],
        out_shape=[sd, sd, sd],
        compiler_params=params(2),
        cost_estimate=cost(8 * hq * n * sp * t * dh, 3 * hq * n * dh * 4),
        name='hist_attn',
    )(q, kv, kv)


def new_kernel(idx_ref, q_ref, k_ref, v_ref, m0_ref, l0_ref, acc0_ref, o_ref, m_ref, l_ref, acc_ref, *, c):
    g, tb, dh = q_ref.shape
    n = k_ref.shape[3]
    r = idx_ref[0]
    half = idx_ref[1]
    q = q_ref[...].reshape(g * tb, dh)
    m_ref[...] = m0_ref[...]
    l_ref[...] = l0_ref[...]
    acc_ref[...] = acc0_ref[...]

    def body(j, _):
        softmax_step(q, k_ref[j, 0, 0], v_ref[j, 0, 0], m_ref, l_ref, acc_ref, c)
        return 0

    lax.fori_loop(0, r, body, 0)
    row0 = half * (n // 2) + pl.program_id(1) * tb

    def diagonal(keys):
        shape = (g, tb, keys)
        ti = lax.broadcasted_iota(jnp.int32, shape, 1).reshape(g * tb, keys) + row0
        ki = lax.broadcasted_iota(jnp.int32, shape, 2).reshape(g * tb, keys)
        softmax_step(q, k_ref[r, 0, 0, :keys], v_ref[r, 0, 0, :keys], m_ref, l_ref, acc_ref, c, mask=ki <= ti)

    @pl.when(half == 0)
    def _():
        diagonal(n // 2)

    @pl.when(half == 1)
    def _():
        diagonal(n)

    den = jnp.sum(l_ref[...], axis=2, keepdims=True)
    o = (acc_ref[...] / den).astype(BF16)
    for j in range(g):
        o_ref[:, j * dh:(j + 1) * dh] = o[j]


def new_attn(idx, q, kv, m, l, acc, c):
    hq, n, dh = q.shape
    sp, _, nk, t, _ = kv.shape
    g = hq // nk
    st = pl.BlockSpec((g, TB, dh), lambda h, i, s: (h, i, 0))
    return pl.pallas_call(
        functools.partial(new_kernel, c=c),
        grid_spec=pltpu.PrefetchScalarGridSpec(
            num_scalar_prefetch=1,
            grid=(nk, n // TB),
            in_specs=[
                st,
                pl.BlockSpec((sp, 1, 1, t, dh), lambda h, i, s: (0, 0, h, 0, 0)),
                pl.BlockSpec((sp, 1, 1, t, dh), lambda h, i, s: (0, 1, h, 0, 0)),
                st, st, st,
            ],
            out_specs=pl.BlockSpec((TB, g * dh), lambda h, i, s: (i, h)),
            scratch_shapes=[pltpu.VMEM((g, TB, dh), F32)] * 3,
        ),
        out_shape=jax.ShapeDtypeStruct((n, hq * dh), BF16),
        compiler_params=params(2),
        cost_estimate=cost(8 * hq * n * sp * t * dh // 2, 3 * hq * n * dh * 4),
        name='new_attn',
    )(idx, q, kv, kv, m, l, acc)


def out_kernel(x_ref, a_ref, b_ref, wa_ref, wb_ref, o_ref):
    y = jnp.dot(a_ref[...], wa_ref[0], preferred_element_type=F32)
    y = y + jnp.dot(b_ref[...], wb_ref[...], preferred_element_type=F32)
    o_ref[...] = x_ref[...] + y.astype(BF16)


def out_proj(l, x, a, b, wa, wb):
    n, d = x.shape
    k = a.shape[1]
    return pl.pallas_call(
        out_kernel,
        grid=(d // OB,),
        in_specs=[
            pl.BlockSpec((n, OB), lambda i: (0, i)),
            pl.BlockSpec((n, k), lambda i: (0, 0)),
            pl.BlockSpec((n, k), lambda i: (0, 0)),
            pl.BlockSpec((1, k, OB), lambda i: (l, 0, i)),
            pl.BlockSpec((k, OB), lambda i: (0, i)),
        ],
        out_specs=pl.BlockSpec((n, OB), lambda i: (0, i)),
        out_shape=jax.ShapeDtypeStruct((n, d), BF16),
        compiler_params=params(),
        cost_estimate=cost(4 * n * k * d, 4 * k * d),
        name='out_proj',
    )(x, a, b, wa, wb)


def mlp_kernel(x_ref, g_ref, wg_ref, wu_ref, wd_ref, o_ref, h_ref, u_ref, a_ref, b_ref, *, nf):
    i = pl.program_id(0)

    def activate():
        a = a_ref[...].astype(F32)
        b = b_ref[...].astype(F32)
        j = jnp.maximum(i - 1, 0)
        u = a * (1.0 / (1.0 + jnp.exp(-a))) * b
        u_ref[:, pl.ds(pl.multiple_of(j * CB, CB), CB)] = u.astype(BF16)

    @pl.when(i == 0)
    def _():
        norm_into(h_ref, x_ref, g_ref)
        a_ref[...] = jnp.zeros_like(a_ref)
        b_ref[...] = jnp.zeros_like(b_ref)

    @pl.when(i < nf)
    def _():
        activate()
        a_ref[...] = jnp.dot(h_ref[...], wg_ref[0], preferred_element_type=F32).astype(BF16)
        b_ref[...] = jnp.dot(h_ref[...], wu_ref[0], preferred_element_type=F32).astype(BF16)

    @pl.when(i == nf)
    def _():
        activate()

    @pl.when(i >= nf)
    def _():
        o_ref[...] = jnp.dot(u_ref[...], wd_ref[0], preferred_element_type=F32)


def mlp(l, x, g, wg, wu, wd):
    n, d = x.shape
    f = wg.shape[-1]
    nf = f // CB
    fi = lambda i: jnp.minimum(i, nf - 1)
    di = lambda i: jnp.maximum(i - nf, 0)
    return pl.pallas_call(
        functools.partial(mlp_kernel, nf=nf),
        grid=(nf + d // DB,),
        in_specs=[
            pl.BlockSpec((n, d), lambda i: (0, 0)),
            pl.BlockSpec((1, 1, d), lambda i: (l, 0, 0)),
            pl.BlockSpec((1, d, CB), lambda i: (l, 0, fi(i))),
            pl.BlockSpec((1, d, CB), lambda i: (l, 0, fi(i))),
            pl.BlockSpec((1, f, DB), lambda i: (l, 0, di(i))),
        ],
        out_specs=pl.BlockSpec((n, DB), lambda i: (0, di(i))),
        out_shape=jax.ShapeDtypeStruct((n, d), F32),
        scratch_shapes=[
            pltpu.VMEM((n, d), BF16), pltpu.VMEM((n, f), BF16),
            pltpu.VMEM((n, CB), BF16), pltpu.VMEM((n, CB), BF16),
        ],
        compiler_params=params(),
        cost_estimate=cost(6 * n * d * f, 6 * d * f),
        name='mlp',
    )(x, g, wg, wu, wd)


def solution(mesh):
    sp = mesh.shape['sp']
    tp = mesh.shape['tp']
    row = ('dp', 'sp')
    kv_spec = P(None, row, 'tp', None)
    col = P(None, None, 'tp')
    rowsplit = P(None, 'tp', None)
    swap_perm = [(0, 1), (1, 0)]

    def swap(t):
        return lax.ppermute(t, 'tp', swap_perm)

    def after(t, *deps):
        return lax.optimization_barrier((t,) + deps)[0]

    def body(x, pos, k_hist, v_hist, wq, wk, wv, wo, wg, wu, wd, g1, g2):
        n, d = x.shape
        layers, _, nk, dh = k_hist.shape
        n2 = n // 2
        c = dh ** -0.5 * LOG2E
        r = lax.axis_index('sp')
        t = lax.axis_index('tp')
        g1 = g1[:, None, :]
        g2 = g2[:, None, :]

        half = dh // 2
        inv = ROPE_THETA ** (-(jnp.arange(half, dtype=F32) * (2.0 / dh)))
        ang = pos.astype(F32)[:, None] * inv
        cs, sn = jnp.cos(ang), jnp.sin(ang)
        cos = jnp.concatenate([cs, cs], axis=-1)
        sin = jnp.concatenate([-sn, sn], axis=-1)

        def own_other(a):
            return (lax.dynamic_slice_in_dim(a, t * n2, n2, axis=0),
                    lax.dynamic_slice_in_dim(a, (1 - t) * n2, n2, axis=0))

        def in_order(own, other, axis):
            both = jnp.concatenate([own, other], axis=axis)
            flip = jnp.concatenate([other, own], axis=axis)
            return jnp.where(t == 0, both, flip)

        cos_s, cos_p = own_other(cos)
        sin_s, sin_p = own_other(sin)
        x_s, x_p = own_other(x)
        idx_s = jnp.stack([r, t]).astype(jnp.int32)
        idx_p = jnp.stack([r, 1 - t]).astype(jnp.int32)

        hist = jnp.stack([k_hist, v_hist], axis=1).transpose(0, 1, 3, 2, 4)
        kq = wo.shape[1] // sp
        ks, vs = [], []
        hist_all = [lax.all_gather(hist[l], 'sp', axis=0) for l in range(layers)]

        def fetch_out(l, start, end):
            piece = lax.dynamic_slice_in_dim(after(wo, start)[l], r * kq, kq, axis=0)
            return after(swap(piece), end)

        def gather_out(piece):
            return lax.all_gather(piece, 'sp', axis=0, tiled=True)

        wo_next = None
        for l in range(layers):
            q_s, kv_s = qkv(l, x_s, g1, cos_s, sin_s, wq, wk, wv, dh)
            if l == 0:
                q_p, kv_p = qkv(l, x_p, g1, cos_p, sin_p, wq, wk, wv, dh)
                st_s = hist_attn(after(q_s, q_p), hist_all[l], c)
                wo_rem = gather_out(fetch_out(l, pos, st_s[0]))
            else:
                st_s = hist_attn(q_s, hist_all[l], c)
                x_p = after(x_p, st_s[0])
                q_p, kv_p = qkv(l, x_p, g1, cos_p, sin_p, wq, wk, wv, dh)
                wo_rem = wo_next
            kv = in_order(kv_s, kv_p, 2)
            ks.append(kv[0])
            vs.append(kv[1])
            kv_all = lax.all_gather(kv, 'sp', axis=0)
            st_p = hist_attn(after(q_p, st_s[0]), hist_all[l], c)
            q_s = after(q_s, st_p[0])
            o_s = new_attn(idx_s, q_s, kv_all, *st_s, c)
            q_p = after(q_p, o_s)
            if l + 1 < layers:
                piece = fetch_out(l + 1, st_s[0], o_s)
                q_p = after(q_p, piece)
                wo_next = gather_out(piece)
            o_p = new_attn(idx_p, q_p, kv_all, *st_p, c)
            r_p = swap(o_s)
            r_s = swap(o_p)
            x_p = out_proj(l, x_p, o_p, r_p, wo, wo_rem)
            part_p = mlp(l, x_p, g2, wg, wu, wd)
            x_s = after(x_s, part_p)
            x_s = out_proj(l, x_s, o_s, r_s, wo, wo_rem)
            part_s = mlp(l, x_s, g2, wg, wu, wd)
            recv = swap(part_p)
            x_s = x_s + (part_s + recv).astype(BF16)
            x_p = swap(x_s)
        x = in_order(x_s, x_p, 0)
        k = jnp.stack(ks).transpose(0, 2, 1, 3)
        v = jnp.stack(vs).transpose(0, 2, 1, 3)
        return x, k, v

    in_specs = (P(row, None), P(row), kv_spec, kv_spec, col, col, col, rowsplit, col, col, rowsplit, P(), P())
    out_specs = (P(row, None), kv_spec, kv_spec)
    return jax.shard_map(body, mesh=mesh, in_specs=in_specs, out_specs=out_specs, check_vma=False)
```

time: 6240 us -> 1900 us (0.30)
  matrix products: 2590 us -> 0 us
  blocking collectives: 2010 us -> 0 us
  Pallas kernels: 0 us -> 1550 us
  other arithmetic: 965 us -> 45.8 us
  local copies, waits for them, and re-layouts: 405 us -> 44.9 us
    dot_general x501 -> x0, matrix products: 2590 us -> none  [the longest x21 921 us: mm(): return jnp.dot(a, b, preferred_element_type=jnp.float32)]
    psum x6 -> x0, blocking collectives: 2010 us -> none  [the longest x3 1010 us: body(): x = x + lax.psum(mm(attn, wo[l]), 'tp').astype(jnp.bfloat16)]
    pallas_call x0 -> x30, Pallas kernels: none -> 1550 us  [the longest x6 755 us: mlp(): pl.pallas_call(functools.partial(mlp_kernel, nf=nf), grid=(nf + d // DB,)...]
    reduce_sum x246 -> x0, other arithmetic: 751 us -> none  [the longest x240 689 us: partial_attn(): return (m, jnp.sum(p, axis=-1), o)]
    unnamed x140 -> x34, local copies, waits for them, and re-layouts: 133 us -> 7.54 us
    all_gather x9, waiting for transfers between devices: 206 us -> 90.3 us  [the longest x3 82.3 us: gather_out(): return lax.all_gather(piece, 'sp', axis=0, tiled=True)]
    ppermute x0 -> x15, waiting for transfers between devices: none -> 105 us  [swap(): return lax.ppermute(t, 'tp', swap_perm)]
    mul x8 -> x0, other arithmetic: 66.4 us -> none  [the longest x3 60.4 us: body(): o_h.reshape(s_tot, kvl, g, dh) * sc[..., None]]
  transfers between devices with their start and end apart: 18 -> 24, of which waited for: 3 -> 7; matrix products, arithmetic and copies ran while one was open for 47% -> 3% of each run, Pallas kernels for 0% -> 80%
where the time goes in v1:
time: 1900 us; the launch traced here: 1890 us
  Pallas kernels  1550 us (82%)
  waiting for transfers between devices  196 us (10%)
  other arithmetic  45.8 us (2%)
  local copies, waits for them, and re-layouts  44.9 us (2%)
  starting transfers between devices  32.9 us (2%)
    pallas_call x6, Pallas kernels, mlp(): pl.pallas_call(functools.partial(mlp_kernel, nf=nf), grid=(nf + d // DB,)...  755 us
    pallas_call x6, Pallas kernels, hist_attn(): pl.pallas_call(functools.partial(hist_kernel, c=c, chunk=min(HCHUNK, t)),...  478 us
    pallas_call x6, Pallas kernels, out_proj(): pl.pallas_call(out_kernel, grid=(d // OB,), in_specs=[pl.BlockSpec((n, OB...  122 us
    pallas_call x6, Pallas kernels, qkv(): pl.pallas_call(functools.partial(qkv_kernel, dh=dh, nk=nk), grid=(nb + 1,...  106 us
    ppermute x15, waiting for transfers between devices, swap(): return lax.ppermute(t, 'tp', swap_perm)  105 us
    pallas_call x6, Pallas kernels, new_attn(): pl.pallas_call(functools.partial(new_kernel, c=c), grid_spec=pltpu.Prefet...  93.2 us
    all_gather x3, waiting for transfers between devices, gather_out(): return lax.all_gather(piece, 'sp', axis=0, tiled=True)  82.3 us
  transfers between devices with their start and end apart: 24, of which 7 were waited for; matrix products, arithmetic and copies ran while one was open for 3% of the time, Pallas kernels for 80%

profile of v1, /device:TPU:0, one launch (start us, length us, event | category | flops | bytes accessed | tf_op | source)
XLA Modules:
  0.0 1887.3 jit_solution(6598040245162716877)
XLA Ops:
  18.5 6.7 constant_dynamic-slice_fusion
  25.2 17.6 qkv.6
  42.9 17.6 qkv.7
  63.0 10.6 slice.38
  79.1 77.2 %hist_attn.6 = (f32[14,512,128]{2,1,0:T(8,128)}, f32[14,512,128]{2,1,0:T(8,128)}, f32[14,512,128]{2,1,0:T(8,128)}) custom-call(bf16[14,512,128]{2,1,0:T(8,128)(2,1)} %get-tuple-element.62.q_ref, bf16[4,2,2,2048,128]{4,3,2,1,0:T(8,128)(2,1)} %all-gather.10.cloned.1.call-done.k_ref.v_ref, bf16[4,2,2,2048,128]{4,3,2,1,0:T(8,128)(2,1)} %all-gather.10.cloned.1.call-done.k_ref.v_ref), custom_call_target="tpu_custom_call" | custom-call | flops 60129542144 | bytes 11010048 | tf_op jit(solution)/shard_map/hist_attn/pallas_call | solution.py:144
  157.0 4.7 slice-done
  162.0 90.4 %hist_attn.7 = (f32[14,512,128]{2,1,0:T(8,128)}, f32[14,512,128]{2,1,0:T(8,128)}, f32[14,512,128]{2,1,0:T(8,128)}) custom-call(bf16[14,512,128]{2,1,0:T(8,128)(2,1)} %get-tuple-element.70.q_ref, bf16[4,2,2,2048,128]{4,3,2,1,0:T(8,128)(2,1)} %all-gather.10.cloned.1.call-done.k_ref.v_ref, bf16[4,2,2,2048,128]{4,3,2,1,0:T(8,128)(2,1)} %all-gather.10.cloned.1.call-done.k_ref.v_ref), custom_call_target="tpu_custom_call" | custom-call | flops 60129542144 | bytes 11010048 | tf_op jit(solution)/shard_map/hist_attn/pallas_call | solution.py:144
  252.4 13.0 new_attn.6.a_ref
  265.4 7.0 collective-permute-start.1
  273.8 18.1 new_attn.7.a_ref
  291.9 13.1 collective-permute-done.1.b_ref
  305.0 20.3 %out_proj.6.x_ref = bf16[512,3584]{1,0:T(8,128)(2,1)} custom-call(bf16[512,3584]{1,0:T(8,128)(2,1)} %get-tuple-element.118.x_ref, bf16[512,1792]{1,0:T(8,128)(2,1)} %new_attn.7.a_ref, bf16[512,1792]{1,0:T(8,128)(2,1)} %collective-permute-done.1.b_ref, bf16[3,1792,3584]{2,1,0:T(8,128)(2,1)} %wa_ref.11, bf16[1792,3584]{1,0:T(8,128)(2,1)} %all-gather.14.cloned.1.call-done.wb_ref), custom_call_target="tpu_custom_call" | custom-call | flops 13153337344 | bytes 25690112 | tf_op jit(solution)/shard_map/out_proj/pallas_call | solution.py:232
  325.4 126.0 %mlp.6 = f32[512,3584]{1,0:T(8,128)} custom-call(bf16[512,3584]{1,0:T(8,128)(2,1)} %out_proj.6.x_ref, bf16[3,1,3584]{2,1,0:T(2,128)(2,1)} %copy.40.g_ref, bf16[3,3584,9472]{2,1,0:T(8,128)(2,1)} %wg_ref.11, bf16[3,3584,9472]{2,1,0:T(8,128)(2,1)} %wu_ref.11, bf16[3,9472,3584]{2,1,0:T(8,128)(2,1)} %wd_ref.11), custom_call_target="tpu_custom_call" | custom-call | flops 104287174656 | bytes 203685888 | tf_op jit(solution)/shard_map/mlp/pallas_call | solution.py:287
  453.7 20.3 %out_proj.7.x_ref = bf16[512,3584]{1,0:T(8,128)(2,1)} custom-call(bf16[512,3584]{1,0:T(8,128)(2,1)} %get-tuple-element.75.x_ref, bf16[512,1792]{1,0:T(8,128)(2,1)} %new_attn.6.a_ref, bf16[512,1792]{1,0:T(8,128)(2,1)} %collective-permute-done.3.b_ref, bf16[3,1792,3584]{2,1,0:T(8,128)(2,1)} %wa_ref.11, bf16[1792,3584]{1,0:T(8,128)(2,1)} %all-gather.14.cloned.1.call-done.wb_ref), custom_call_target="tpu_custom_call" | custom-call | flops 13153337344 | bytes 25690112 | tf_op jit(solution)/shard_map/out_proj/pallas_call | solution.py:232
  474.0 126.7 %mlp.7 = f32[512,3584]{1,0:T(8,128)} custom-call(bf16[512,3584]{1,0:T(8,128)(2,1)} %out_proj.7.x_ref, bf16[3,1,3584]{2,1,0:T(2,128)(2,1)} %copy.40.g_ref, bf16[3,3584,9472]{2,1,0:T(8,128)(2,1)} %wg_ref.11, bf16[3,3584,9472]{2,1,0:T(8,128)(2,1)} %wu_ref.11, bf16[3,9472,3584]{2,1,0:T(8,128)(2,1)} %wd_ref.11), custom_call_target="tpu_custom_call" | custom-call | flops 104287174656 | bytes 203685888 | tf_op jit(solution)/shard_map/mlp/pallas_call | solution.py:287
  600.8 9.0 fusion.x_ref
  609.8 17.5 qkv.8
  627.3 77.6 %hist_attn.8 = (f32[14,512,128]{2,1,0:T(8,128)}, f32[14,512,128]{2,1,0:T(8,128)}, f32[14,512,128]{2,1,0:T(8,128)}) custom-call(bf16[14,512,128]{2,1,0:T(8,128)(2,1)} %get-tuple-element.82.q_ref, bf16[4,2,2,2048,128]{4,3,2,1,0:T(8,128)(2,1)} %all-gather.16.cloned.1.call-done.k_ref.v_ref, bf16[4,2,2,2048,128]{4,3,2,1,0:T(8,128)(2,1)} %all-gather.16.cloned.1.call-done.k_ref.v_ref), custom_call_target="tpu_custom_call" | custom-call | flops 60129542144 | bytes 11010048 | tf_op jit(solution)/shard_map/hist_attn/pallas_call | solution.py:144
  704.9 17.6 qkv.9
  725.7 4.6 slice-done.1
  732.5 77.6 %hist_attn.9 = (f32[14,512,128]{2,1,0:T(8,128)}, f32[14,512,128]{2,1,0:T(8,128)}, f32[14,512,128]{2,1,0:T(8,128)}) custom-call(bf16[14,512,128]{2,1,0:T(8,128)(2,1)} %get-tuple-element.90.q_ref, bf16[4,2,2,2048,128]{4,3,2,1,0:T(8,128)(2,1)} %all-gather.16.cloned.1.call-done.k_ref.v_ref, bf16[4,2,2,2048,128]{4,3,2,1,0:T(8,128)(2,1)} %all-gather.16.cloned.1.call-done.k_ref.v_ref), custom_call_target="tpu_custom_call" | custom-call | flops 60129542144 | bytes 11010048 | tf_op jit(solution)/shard_map/hist_attn/pallas_call | solution.py:144
  810.2 12.9 new_attn.8.a_ref
  823.1 5.2 collective-permute-start.7
  828.4 18.1 new_attn.9.a_ref
  846.5 37.0 %all-gather.20.cloned.1.call-done.wb_ref = bf16[1792,3584]{1,0:T(8,128)(2,1)} async-done(((bf16[448,3584]{1,0:T(8,128)(2,1)}), bf16[1792,3584]{1,0:T(8,128)(2,1)}) %all-gather.20.cloned.1.call-update) | async-done | bytes 12845072 | tf_op jit(solution)/shard_map/all_gather | solution.py:366
  883.5 20.2 %out_proj.8.x_ref = bf16[512,3584]{1,0:T(8,128)(2,1)} custom-call(bf16[512,3584]{1,0:T(8,128)(2,1)} %collective-permute-done.5.x_ref, bf16[512,1792]{1,0:T(8,128)(2,1)} %new_attn.9.a_ref, bf16[512,1792]{1,0:T(8,128)(2,1)} %collective-permute-done.7.b_ref, bf16[3,1792,3584]{2,1,0:T(8,128)(2,1)} %wa_ref.11, bf16[1792,3584]{1,0:T(8,128)(2,1)} %all-gather.20.cloned.1.call-done.wb_ref), custom_call_target="tpu_custom_call" | custom-call | flops 13153337344 | bytes 25690112 | tf_op jit(solution)/shard_map/out_proj/pallas_call | solution.py:232
  903.8 125.1 %mlp.8 = f32[512,3584]{1,0:T(8,128)} custom-call(bf16[512,3584]{1,0:T(8,128)(2,1)} %out_proj.8.x_ref, bf16[3,1,3584]{2,1,0:T(2,128)(2,1)} %copy.40.g_ref, bf16[3,3584,9472]{2,1,0:T(8,128)(2,1)} %wg_ref.11, bf16[3,3584,9472]{2,1,0:T(8,128)(2,1)} %wu_ref.11, bf16[3,9472,3584]{2,1,0:T(8,128)(2,1)} %wd_ref.11), custom_call_target="tpu_custom_call" | custom-call | flops 104287174656 | bytes 203685888 | tf_op jit(solution)/shard_map/mlp/pallas_call | solution.py:287
  1030.4 20.3 %out_proj.9.x_ref = bf16[512,3584]{1,0:T(8,128)(2,1)} custom-call(bf16[512,3584]{1,0:T(8,128)(2,1)} %fusion.x_ref, bf16[512,1792]{1,0:T(8,128)(2,1)} %new_attn.8.a_ref, bf16[512,1792]{1,0:T(8,128)(2,1)} %collective-permute-done.8.b_ref, bf16[3,1792,3584]{2,1,0:T(8,128)(2,1)} %wa_ref.11, bf16[1792,3584]{1,0:T(8,128)(2,1)} %all-gather.20.cloned.1.call-done.wb_ref), custom_call_target="tpu_custom_call" | custom-call | flops 13153337344 | bytes 25690112 | tf_op jit(solution)/shard_map/out_proj/pallas_call | solution.py:232
  1050.7 125.8 %mlp.9 = f32[512,3584]{1,0:T(8,128)} custom-call(bf16[512,3584]{1,0:T(8,128)(2,1)} %out_proj.9.x_ref, bf16[3,1,3584]{2,1,0:T(2,128)(2,1)} %copy.40.g_ref, bf16[3,3584,9472]{2,1,0:T(8,128)(2,1)} %wg_ref.11, bf16[3,3584,9472]{2,1,0:T(8,128)(2,1)} %wu_ref.11, bf16[3,9472,3584]{2,1,0:T(8,128)(2,1)} %wd_ref.11), custom_call_target="tpu_custom_call" | custom-call | flops 104287174656 | bytes 203685888 | tf_op jit(solution)/shard_map/mlp/pallas_call | solution.py:287
  1176.5 8.5 collective-permute-done.9
  1185.1 8.9 fusion.1.x_ref
  1195.5 17.5 qkv.10
  1213.0 77.6 %hist_attn.10 = (f32[14,512,128]{2,1,0:T(8,128)}, f32[14,512,128]{2,1,0:T(8,128)}, f32[14,512,128]{2,1,0:T(8,128)}) custom-call(bf16[14,512,128]{2,1,0:T(8,128)(2,1)} %get-tuple-element.100.q_ref, bf16[4,2,2,2048,128]{4,3,2,1,0:T(8,128)(2,1)} %all-gather.22.cloned.1.call-done.k_ref.v_ref, bf16[4,2,2,2048,128]{4,3,2,1,0:T(8,128)(2,1)} %all-gather.22.cloned.1.call-done.k_ref.v_ref), custom_call_target="tpu_custom_call" | custom-call | flops 60129542144 | bytes 11010048 | tf_op jit(solution)/shard_map/hist_attn/pallas_call | solution.py:144
  1290.6 17.6 qkv.11
  1311.5 77.5 %hist_attn.11 = (f32[14,512,128]{2,1,0:T(8,128)}, f32[14,512,128]{2,1,0:T(8,128)}, f32[14,512,128]{2,1,0:T(8,128)}) custom-call(bf16[14,512,128]{2,1,0:T(8,128)(2,1)} %get-tuple-element.105.q_ref, bf16[4,2,2,2048,128]{4,3,2,1,0:T(8,128)(2,1)} %all-gather.22.cloned.1.call-done.k_ref.v_ref, bf16[4,2,2,2048,128]{4,3,2,1,0:T(8,128)(2,1)} %all-gather.22.cloned.1.call-done.k_ref.v_ref), custom_call_target="tpu_custom_call" | custom-call | flops 60129542144 | bytes 11010048 | tf_op jit(solution)/shard_map/hist_attn/pallas_call | solution.py:144
  1389.0 7.9 all-gather.24.cloned.1.call-done.k_ref.v_ref
  1396.9 12.9 new_attn.10.a_ref
  1409.9 6.6 collective-permute-start.11
  1416.5 18.1 new_attn.11.a_ref
  1434.6 45.4 %all-gather.26.cloned.1.call-done.wb_ref = bf16[1792,3584]{1,0:T(8,128)(2,1)} async-done(((bf16[448,3584]{1,0:T(8,128)(2,1)}), bf16[1792,3584]{1,0:T(8,128)(2,1)}) %all-gather.26.cloned.1.call-update) | async-done | bytes 12845072 | tf_op jit(solution)/shard_map/all_gather | solution.py:366
  1481.2 20.2 %out_proj.10.x_ref = bf16[512,3584]{1,0:T(8,128)(2,1)} custom-call(bf16[512,3584]{1,0:T(8,128)(2,1)} %collective-permute-done.10.x_ref, bf16[512,1792]{1,0:T(8,128)(2,1)} %new_attn.11.a_ref, bf16[512,1792]{1,0:T(8,128)(2,1)} %copy-done.12, bf16[3,1792,3584]{2,1,0:T(8,128)(2,1)} %wa_ref.11, bf16[1792,3584]{1,0:T(8,128)(2,1)} %all-gather.26.cloned.1.call-done.wb_ref), custom_call_target="tpu_custom_call" | custom-call | flops 13153337344 | bytes 25690112 | tf_op jit(solution)/shard_map/out_proj/pallas_call | solution.py:232
  1501.4 125.1 %mlp.10 = f32[512,3584]{1,0:T(8,128)} custom-call(bf16[512,3584]{1,0:T(8,128)(2,1)} %out_proj.10.x_ref, bf16[3,1,3584]{2,1,0:T(2,128)(2,1)} %copy.40.g_ref, bf16[3,3584,9472]{2,1,0:T(8,128)(2,1)} %wg_ref.11, bf16[3,3584,9472]{2,1,0:T(8,128)(2,1)} %wu_ref.11, bf16[3,9472,3584]{2,1,0:T(8,128)(2,1)} %wd_ref.11), custom_call_target="tpu_custom_call" | custom-call | flops 104287174656 | bytes 203685888 | tf_op jit(solution)/shard_map/mlp/pallas_call | solution.py:287
  1628.0 20.3 %out_proj.11.x_ref = bf16[512,3584]{1,0:T(8,128)(2,1)} custom-call(bf16[512,3584]{1,0:T(8,128)(2,1)} %fusion.1.x_ref, bf16[512,1792]{1,0:T(8,128)(2,1)} %new_attn.10.a_ref, bf16[512,1792]{1,0:T(8,128)(2,1)} %collective-permute-done.12.b_ref, bf16[3,1792,3584]{2,1,0:T(8,128)(2,1)} %wa_ref.11, bf16[1792,3584]{1,0:T(8,128)(2,1)} %all-gather.26.cloned.1.call-done.wb_ref), custom_call_target="tpu_custom_call" | custom-call | flops 13153337344 | bytes 25690112 | tf_op jit(solution)/shard_map/out_proj/pallas_call | solution.py:232
  1648.3 125.8 %mlp.11 = f32[512,3584]{1,0:T(8,128)} custom-call(bf16[512,3584]{1,0:T(8,128)(2,1)} %out_proj.11.x_ref, bf16[3,1,3584]{2,1,0:T(2,128)(2,1)} %copy.40.g_ref, bf16[3,3584,9472]{2,1,0:T(8,128)(2,1)} %wg_ref.11, bf16[3,3584,9472]{2,1,0:T(8,128)(2,1)} %wu_ref.11, bf16[3,9472,3584]{2,1,0:T(8,128)(2,1)} %wd_ref.11), custom_call_target="tpu_custom_call" | custom-call | flops 104287174656 | bytes 203685888 | tf_op jit(solution)/shard_map/mlp/pallas_call | solution.py:287
  1774.2 12.5 collective-permute-done.13
  1786.7 8.9 fusion.2
  1806.0 70.4 %collective-permute-done.14 = bf16[512,3584]{1,0:T(8,128)(2,1)S(1)} collective-permute-done((bf16[512,3584]{1,0:T(8,128)(2,1)}, bf16[512,3584]{1,0:T(8,128)(2,1)S(1)}, u32[]{:S(2)}, u32[]{:S(2)}) %collective-permute-start.14) | collective-permute-done | bytes 3670048 | tf_op jit(solution)/shard_map/ppermute | solution.py:319
  1876.4 4.1 maximum_select_fusion
  (108 shorter events, 48.5 us)
Async XLA Ops:
  7.2 71.9 %all-gather.10.cloned.1.call-start = ((), (), s32[]{:S(2)}) async-start(), calls=%async_computation | async-start | bytes 10485760 | tf_op jit(solution)/shard_map/all_gather | solution.py:359
  11.7 2.9 copy-start.13
  11.7 3.6 copy-start.15
  14.5 237.9 %all-gather.12.cloned.1.call-start = ((), (), s32[]{:S(2)}) async-start(), calls=%async_computation.1 | async-start | bytes 5242880 | tf_op jit(solution)/shard_map/all_gather | solution.py:383
  42.8 17.6 copy-start.4
  63.0 242.0 %all-gather.14.cloned.1.call-start = ((), (), s32[]{:S(2)}) async-start(), calls=%async_computation.2 | async-start | bytes 16056320 | tf_op jit(solution)/shard_map/all_gather | solution.py:366
  75.7 80.6 %collective-permute-start.2 = (bf16[448,3584]{1,0:T(8,128)(2,1)S(1)}, bf16[448,3584]{1,0:T(8,128)(2,1)}, u32[]{:S(2)}, u32[]{:S(2)}) collective-permute-start(bf16[448,3584]{1,0:T(8,128)(2,1)S(1)} %dynamic-slice_bitcast_fusion.1), channel_id=1, source_target_pairs={{0,4},{4,0},{1,5},{5,1},{2,6},{6,2},{3,7},{7,3}} | collective-permute-start | bytes 9633800 | tf_op jit(solution)/shard_map/ppermute | solution.py:319
  156.3 471.0 %all-gather.16.cloned.1.call-start = ((), (), s32[]{:S(2)}) async-start(), calls=%async_computation.3 | async-start | bytes 10485760 | tf_op jit(solution)/shard_map/all_gather | solution.py:359
  157.0 4.7 slice-start
  161.9 111.9 %collective-permute-start = (bf16[448,3584]{1,0:T(8,128)(2,1)S(1)}, bf16[448,3584]{1,0:T(8,128)(2,1)}, u32[]{:S(2)}, u32[]{:S(2)}) collective-permute-start(bf16[448,3584]{1,0:T(8,128)(2,1)S(1)} %dynamic-slice_bitcast_fusion.2), channel_id=1, source_target_pairs={{0,4},{4,0},{1,5},{5,1},{2,6},{6,2},{3,7},{7,3}} | collective-permute-start | bytes 9633800 | tf_op jit(solution)/shard_map/ppermute | solution.py:319
  252.4 20.1 %copy-start.14 = (bf16[3,3584]{1,0:T(4,128)(2,1)S(1)}, bf16[3,3584]{1,0:T(4,128)(2,1)}, u32[]{:S(2)}) copy-start(bf16[3,3584]{1,0:T(4,128)(2,1)} %param.25) | copy-start | bytes 64516
  265.4 39.6 %collective-permute-start.1 = (bf16[512,1792]{1,0:T(8,128)(2,1)}, bf16[512,1792]{1,0:T(8,128)(2,1)}, u32[]{:S(2)}, u32[]{:S(2)}) collective-permute-start(bf16[512,1792]{1,0:T(8,128)(2,1)} %new_attn.6.a_ref), channel_id=1, source_target_pairs={{0,4},{4,0},{1,5},{5,1},{2,6},{6,2},{3,7},{7,3}} | collective-permute-start | bytes 5505032 | tf_op jit(solution)/shard_map/ppermute | solution.py:319
  272.4 537.7 %all-gather.18.cloned.1.call-start = ((), (), s32[]{:S(2)}) async-start(), calls=%async_computation.4 | async-start | bytes 5242880 | tf_op jit(solution)/shard_map/all_gather | solution.py:383
  291.9 161.8 %collective-permute-start.3 = (bf16[512,1792]{1,0:T(8,128)(2,1)}, bf16[512,1792]{1,0:T(8,128)(2,1)}, u32[]{:S(2)}, u32[]{:S(2)}) collective-permute-start(bf16[512,1792]{1,0:T(8,128)(2,1)} %new_attn.7.a_ref), channel_id=1, source_target_pairs={{0,4},{4,0},{1,5},{5,1},{2,6},{6,2},{3,7},{7,3}} | collective-permute-start | bytes 5505032 | tf_op jit(solution)/shard_map/ppermute | solution.py:319
  451.4 149.4 %collective-permute-start.4 = (f32[512,3584]{1,0:T(8,128)}, f32[512,3584]{1,0:T(8,128)}, u32[]{:S(2)}, u32[]{:S(2)}) collective-permute-start(f32[512,3584]{1,0:T(8,128)} %mlp.6), channel_id=1, source_target_pairs={{0,4},{4,0},{1,5},{5,1},{2,6},{6,2},{3,7},{7,3}} | collective-permute-start | bytes 22020104 | tf_op jit(solution)/shard_map/ppermute | solution.py:319
  474.0 126.7 %copy-start.1 = (bf16[512,3584]{1,0:T(8,128)(2,1)S(1)}, bf16[512,3584]{1,0:T(8,128)(2,1)}, u32[]{:S(2)}) copy-start(bf16[512,3584]{1,0:T(8,128)(2,1)} %out_proj.7.x_ref) | copy-start | bytes 11010052
  609.7 95.2 %collective-permute-start.5 = (bf16[512,3584]{1,0:T(8,128)(2,1)}, bf16[512,3584]{1,0:T(8,128)(2,1)}, u32[]{:S(2)}, u32[]{:S(2)}) collective-permute-start(bf16[512,3584]{1,0:T(8,128)(2,1)} %fusion.x_ref), channel_id=1, source_target_pairs={{0,4},{4,0},{1,5},{5,1},{2,6},{6,2},{3,7},{7,3}} | collective-permute-start | bytes 11010056 | tf_op jit(solution)/shard_map/ppermute | solution.py:319
  704.9 17.6 copy-start.6
  725.0 158.5 %all-gather.20.cloned.1.call-start = ((), (), s32[]{:S(2)}) async-start(), calls=%async_computation.5 | async-start | bytes 16056320 | tf_op jit(solution)/shard_map/all_gather | solution.py:366
  725.6 487.4 %all-gather.22.cloned.1.call-start = ((), (), s32[]{:S(2)}) async-start(), calls=%async_computation.6 | async-start | bytes 10485760 | tf_op jit(solution)/shard_map/all_gather | solution.py:359
  725.6 4.7 slice-start.1
  730.5 97.9 %collective-permute-start.6 = (bf16[448,3584]{1,0:T(8,128)(2,1)S(1)}, bf16[448,3584]{1,0:T(8,128)(2,1)}, u32[]{:S(2)}, u32[]{:S(2)}) collective-permute-start(bf16[448,3584]{1,0:T(8,128)(2,1)S(1)} %dynamic-slice_bitcast_fusion), channel_id=1, source_target_pairs={{0,4},{4,0},{1,5},{5,1},{2,6},{6,2},{3,7},{7,3}} | collective-permute-start | bytes 9633800 | tf_op jit(solution)/shard_map/ppermute | solution.py:319
  823.1 60.4 %collective-permute-start.7 = (bf16[512,1792]{1,0:T(8,128)(2,1)}, bf16[512,1792]{1,0:T(8,128)(2,1)}, u32[]{:S(2)}, u32[]{:S(2)}) collective-permute-start(bf16[512,1792]{1,0:T(8,128)(2,1)} %new_attn.8.a_ref), channel_id=1, source_target_pairs={{0,4},{4,0},{1,5},{5,1},{2,6},{6,2},{3,7},{7,3}} | collective-permute-start | bytes 5505032 | tf_op jit(solution)/shard_map/ppermute | solution.py:319
  828.4 568.6 %all-gather.24.cloned.1.call-start = ((), (), s32[]{:S(2)}) async-start(), calls=%async_computation.7 | async-start | bytes 5242880 | tf_op jit(solution)/shard_map/all_gather | solution.py:383
  846.5 183.9 %collective-permute-start.8 = (bf16[512,1792]{1,0:T(8,128)(2,1)}, bf16[512,1792]{1,0:T(8,128)(2,1)}, u32[]{:S(2)}, u32[]{:S(2)}) collective-permute-start(bf16[512,1792]{1,0:T(8,128)(2,1)} %new_attn.9.a_ref), channel_id=1, source_target_pairs={{0,4},{4,0},{1,5},{5,1},{2,6},{6,2},{3,7},{7,3}} | collective-permute-start | bytes 5505032 | tf_op jit(solution)/shard_map/ppermute | solution.py:319
  1028.9 156.1 %collective-permute-start.9 = (f32[512,3584]{1,0:T(8,128)}, f32[512,3584]{1,0:T(8,128)}, u32[]{:S(2)}, u32[]{:S(2)}) collective-permute-start(f32[512,3584]{1,0:T(8,128)} %mlp.8), channel_id=1, source_target_pairs={{0,4},{4,0},{1,5},{5,1},{2,6},{6,2},{3,7},{7,3}} | collective-permute-start | bytes 22020104 | tf_op jit(solution)/shard_map/ppermute | solution.py:319
  1050.7 134.4 %copy-start.2 = (bf16[512,3584]{1,0:T(8,128)(2,1)S(1)}, bf16[512,3584]{1,0:T(8,128)(2,1)}, u32[]{:S(2)}) copy-start(bf16[512,3584]{1,0:T(8,128)(2,1)} %out_proj.9.x_ref) | copy-start | bytes 11010052
  1194.0 96.6 %collective-permute-start.10 = (bf16[512,3584]{1,0:T(8,128)(2,1)}, bf16[512,3584]{1,0:T(8,128)(2,1)}, u32[]{:S(2)}, u32[]{:S(2)}) collective-permute-start(bf16[512,3584]{1,0:T(8,128)(2,1)} %fusion.1.x_ref), channel_id=1, source_target_pairs={{0,4},{4,0},{1,5},{5,1},{2,6},{6,2},{3,7},{7,3}} | collective-permute-start | bytes 11010056 | tf_op jit(solution)/shard_map/ppermute | solution.py:319
  1290.6 17.6 copy-start.9
  1310.7 169.2 %all-gather.26.cloned.1.call-start = ((), (), s32[]{:S(2)}) async-start(), calls=%async_computation.8 | async-start | bytes 16056320 | tf_op jit(solution)/shard_map/all_gather | solution.py:366
  1409.9 70.1 %collective-permute-start.11 = (bf16[512,1792]{1,0:T(8,128)(2,1)}, bf16[512,1792]{1,0:T(8,128)(2,1)S(1)}, u32[]{:S(2)}, u32[]{:S(2)}) collective-permute-start(bf16[512,1792]{1,0:T(8,128)(2,1)} %new_attn.10.a_ref), channel_id=1, source_target_pairs={{0,4},{4,0},{1,5},{5,1},{2,6},{6,2},{3,7},{7,3}} | collective-permute-start | bytes 5505032 | tf_op jit(solution)/shard_map/ppermute | solution.py:319
  1434.6 193.4 %collective-permute-start.12 = (bf16[512,1792]{1,0:T(8,128)(2,1)}, bf16[512,1792]{1,0:T(8,128)(2,1)}, u32[]{:S(2)}, u32[]{:S(2)}) collective-permute-start(bf16[512,1792]{1,0:T(8,128)(2,1)} %new_attn.11.a_ref), channel_id=1, source_target_pairs={{0,4},{4,0},{1,5},{5,1},{2,6},{6,2},{3,7},{7,3}} | collective-permute-start | bytes 5505032 | tf_op jit(solution)/shard_map/ppermute | solution.py:319
  1480.0 1.2 copy-start.12
  1626.6 160.1 %collective-permute-start.13 = (f32[512,3584]{1,0:T(8,128)}, f32[512,3584]{1,0:T(8,128)}, u32[]{:S(2)}, u32[]{:S(2)}) collective-permute-start(f32[512,3584]{1,0:T(8,128)} %mlp.10), channel_id=1, source_target_pairs={{0,4},{4,0},{1,5},{5,1},{2,6},{6,2},{3,7},{7,3}} | collective-permute-start | bytes 22020104 | tf_op jit(solution)/shard_map/ppermute | solution.py:319
  1648.3 138.4 %copy-start = (bf16[512,3584]{1,0:T(8,128)(2,1)S(1)}, bf16[512,3584]{1,0:T(8,128)(2,1)}, u32[]{:S(2)}) copy-start(bf16[512,3584]{1,0:T(8,128)(2,1)} %out_proj.11.x_ref) | copy-start | bytes 11010052
  1774.2 23.0 %copy-start.5 = (bf16[2,2,512,128]{3,2,1,0:T(8,128)(2,1)S(1)}, bf16[2,2,512,128]{3,2,1,0:T(8,128)(2,1)}, u32[]{:S(2)}) copy-start(bf16[2,2,512,128]{3,2,1,0:T(8,128)(2,1)} %get-tuple-element.64) | copy-start | bytes 1572868
  1795.7 3.0 copy-start.7
  1795.7 3.1 copy-start.8
  1795.7 80.7 %collective-permute-start.14 = (bf16[512,3584]{1,0:T(8,128)(2,1)}, bf16[512,3584]{1,0:T(8,128)(2,1)S(1)}, u32[]{:S(2)}, u32[]{:S(2)}) collective-permute-start(bf16[512,3584]{1,0:T(8,128)(2,1)} %fusion.2), channel_id=1, source_target_pairs={{0,4},{4,0},{1,5},{5,1},{2,6},{6,2},{3,7},{7,3}} | collective-permute-start | bytes 11010056 | tf_op jit(solution)/shard_map/ppermute | solution.py:319
  1798.6 1.0 copy-start.10
  1798.6 1.2 copy-start.11
  1803.1 73.3 %copy-start.3 = (bf16[512,3584]{1,0:T(8,128)(2,1)S(1)}, bf16[512,3584]{1,0:T(8,128)(2,1)}, u32[]{:S(2)}) copy-start(bf16[512,3584]{1,0:T(8,128)(2,1)} %fusion.2) | copy-start | bytes 11010052
Sparse Core Ops, SparseCore 0:
  14.6 58.5 all-gather.9
  75.3 31.4 all-gather.11
  156.4 81.4 all-gather.13
  272.5 83.4 all-gather.15
  725.1 75.4 all-gather.17
  802.0 81.4 all-gather.19
  885.0 70.4 all-gather.21
  1310.8 86.0 all-gather.23
  1398.4 81.4 all-gather.25
